TPU v7x, 32 devices: a whole 2x2x4 slice. The times are simulated.
32 devices in a mesh: grp: 2 (over y), kv: 8 (over z, core), hd: 2 (over x), sub: 1.
Axes of the slice: x: 2, y: 2, z: 4, core: 2. Of those that a mesh axis runs over, the one named last changes fastest.
Arguments:
- queries: bfloat16 [256, 8192], P(('grp', 'kv'), 'hd'), parts along dimension 0, may hold values from -12 to 12
- prompt_of: int32 [256, 1], P('grp'), parts along dimension 0, may hold values from 0 to 1; in each aligned block of 16 rows (0 to 15, 16 to 31, ...) at most 8 rows name the same one
- prompt_len: int32 [4], P('grp'), parts along dimension 0, may hold values from 3072 to 4096
- suffix_len: int32 [256], P(('grp', 'kv')), parts along dimension 0, may hold values from 0 to 512
- page_table: int32 [256, 8], P(('grp', 'kv'), 'sub'), parts along dimension 0, may hold values from 0 to 127, as said below
- prompt_keys: bfloat16 [16384, 1024], P(('grp', 'kv', 'sub'), 'hd'), parts along dimension 0, may hold values from -14 to 14
- shared_prompt_values: bfloat16 [16384, 1024], P(('grp', 'kv', 'sub'), 'hd'), parts along dimension 0, may hold values from -6 to 6
- suffix_pool_keys: bfloat16 [2048, 64, 1024], P(('grp', 'kv', 'sub'), None, 'hd'), parts along dimension 0, may hold values from -14 to 14
- suffix_pool_values: bfloat16 [2048, 64, 1024], P(('grp', 'kv', 'sub'), None, 'hd'), parts along dimension 0, may hold values from -6 to 6
Outputs:
- attended: float32 [256, 8192], P(('grp', 'kv'), 'hd'), parts along dimension 0
There are 2 independent parts, one for each index of `grp`. A program takes and returns all parts, laid end to end along the dimension named above; each array names one. Nothing has to cross between parts.
Inputs may be any that keep to these rules, and one draw needn't show every extreme that they name: `prompt_of`: in each aligned block of 16 rows (the sequences of one index of kv), every prompt is named by exactly 8 rows. `page_table`: for each index k of kv and s of sub, the entries in rows k * 16 to (k + 1) * 16 - 1 and columns s * 8 to (s + 1) * 8 - 1 are a permutation of 0 to 127.
All inputs are finite; a program needn't handle non-finite values.
Results may differ from a plain program's by a relative error of at most 0.0011.
Values may be sent and summed in bfloat16 or wider, within the bound.
A program may use at most 128 MiB of HBM per device.

v0:
```python
import functools
import math

import jax
import jax.numpy as jnp
from jax import lax
from jax.experimental import pallas as pl
from jax.experimental.pallas import tpu as pltpu
from jax.sharding import PartitionSpec as P

HEAD_SIZE = 128


NEGATIVE = -1e30


def joined(value, axis, combine):
    everything = jax.tree.map(lambda part: lax.all_gather(part, axis), value)
    leading = jax.tree.map(lambda part: part[0], everything)

    def hop(k, so_far):
        return combine(so_far, jax.tree.map(lambda part: part[k], everything))

    return lax.fori_loop(1, lax.axis_size(axis), hop, leading)


def attend_block(sent_rows, key_block, value_block, lower_bound, upper_bound, first_position):
    row_count = sent_rows.shape[0]
    key_count = key_block.shape[0]
    kv_local = key_block.shape[1] // HEAD_SIZE
    query_group_size = sent_rows.shape[1] // (HEAD_SIZE * kv_local)
    position = first_position + jnp.arange(key_count, dtype=jnp.int32)
    key_mask = (position[None, :] >= lower_bound[:, None]) & (
        position[None, :] < upper_bound[:, None]
    )
    key_mask = key_mask[:, None, :]
    score_scale = 1.0 / math.sqrt(HEAD_SIZE)
    blended_parts = []
    lse_parts = []
    for kv_head in range(kv_local):
        low_column = kv_head * query_group_size * HEAD_SIZE
        head_query = sent_rows[:, low_column : low_column + query_group_size * HEAD_SIZE].reshape(
            row_count * query_group_size, HEAD_SIZE
        )
        head_keys = key_block[:, kv_head * HEAD_SIZE : (kv_head + 1) * HEAD_SIZE]
        head_values = value_block[:, kv_head * HEAD_SIZE : (kv_head + 1) * HEAD_SIZE]
        scores = lax.dot_general(
            head_query, head_keys, (((1,), (1,)), ((), ())), preferred_element_type=jnp.float32
        )
        scores = (scores * score_scale).reshape(row_count, query_group_size, key_count)
        scores = jnp.where(key_mask, scores, NEGATIVE)
        row_max = jnp.max(scores, axis=2, keepdims=True)
        weights = jnp.where(key_mask, jnp.exp(scores - row_max), 0.0)
        totals = jnp.maximum(jnp.sum(weights, axis=2), 1.0)
        weighted = jnp.dot(
            weights.astype(jnp.bfloat16).reshape(row_count * query_group_size, key_count),
            head_values,
            preferred_element_type=jnp.float32,
        )
        weighted = weighted.reshape(row_count, query_group_size, HEAD_SIZE) / totals[:, :, None]
        blended_parts.append(weighted.reshape(row_count, query_group_size * HEAD_SIZE))
        lse_parts.append(row_max[:, :, 0] + jnp.log(totals))
    return (jnp.concatenate(blended_parts, axis=1), jnp.concatenate(lse_parts, axis=1))


def combine_halves(earlier, later):
    joint_max = jnp.maximum(earlier[0], later[0])
    left_factor = jnp.exp(earlier[0] - joint_max)
    right_factor = jnp.exp(later[0] - joint_max)
    totals = earlier[1] * left_factor + later[1] * right_factor
    blended = earlier[2] * left_factor[:, :, None] + later[2] * right_factor[:, :, None]
    return (joint_max, totals, blended)


def shards(
    queries,
    prompt_of,
    prompt_len,
    suffix_len,
    page_table,
    prompt_keys,
    shared_prompt_values,
    suffix_pool_keys,
    suffix_pool_values,
):
    kv_count = lax.axis_size("kv")
    sub_count = lax.axis_size("sub")
    kv_index = lax.axis_index("kv")
    sub_index = lax.axis_index("sub")
    seq_local = queries.shape[0]
    row_width = queries.shape[1]
    heads_local = row_width // HEAD_SIZE
    cache_local = prompt_keys.shape[0]
    kv_reach = sub_count * cache_local
    prompt_count = prompt_len.shape[0]
    prompt_starts = jnp.cumsum(prompt_len) - prompt_len
    prompt_ends = prompt_starts + prompt_len
    prompt_labels = jnp.arange(prompt_count, dtype=jnp.int32)
    range_low = jnp.arange(kv_count, dtype=jnp.int32) * kv_reach
    intersections = (prompt_starts[None, :] < range_low[:, None] + kv_reach) & (
        prompt_ends[None, :] > range_low[:, None]
    )
    later_slot = prompt_starts[None, :] > range_low[:, None]
    first_position = (kv_index * sub_count + sub_index) * cache_local
    most_rows = seq_local // prompt_count
    owned_prompt = lax.dynamic_slice_in_dim(prompt_of[:, 0], kv_index * seq_local, seq_local)
    prompt_hits = owned_prompt[:, None] == prompt_labels[None, :]
    hit_counts = prompt_hits.astype(jnp.int32)
    ranks = jnp.sum((jnp.cumsum(hit_counts, axis=0) - hit_counts) * hit_counts, axis=1)
    seq_intersection = jnp.any(intersections[:, None, :] & prompt_hits[None, :, :], axis=2)
    seq_later = jnp.any(later_slot[:, None, :] & prompt_hits[None, :, :], axis=2).astype(jnp.int32)
    slot_labels = jnp.arange(2, dtype=jnp.int32)
    rank_labels = jnp.arange(most_rows, dtype=jnp.int32)
    selector = seq_intersection[:, None, None, :] & (
        seq_later[:, None, None, :] == slot_labels[None, :, None, None]
    )
    selector = selector & (ranks[None, None, None, :] == rank_labels[None, None, :, None])
    selector = selector.reshape(kv_count * 2 * most_rows, seq_local)
    outgoing = jnp.dot(
        selector.astype(jnp.bfloat16), queries, preferred_element_type=jnp.float32
    ).astype(jnp.bfloat16)
    incoming = lax.all_to_all(
        outgoing.reshape(kv_count, 2 * most_rows, row_width),
        "kv",
        split_axis=0,
        concat_axis=0,
        tiled=True,
    )
    mine_intersection = lax.dynamic_index_in_dim(intersections, kv_index, 0, keepdims=False)
    mine_later = lax.dynamic_index_in_dim(later_slot, kv_index, 0, keepdims=False).astype(jnp.int32)
    chosen = mine_intersection[None, :] & (mine_later[None, :] == slot_labels[:, None])
    slot_low = jnp.sum(jnp.where(chosen, prompt_starts[None, :], 0), axis=1)
    slot_high = jnp.sum(jnp.where(chosen, prompt_ends[None, :], 0), axis=1)
    lower_bound = jnp.broadcast_to(
        jnp.repeat(slot_low, most_rows)[None, :], (kv_count, 2 * most_rows)
    ).reshape(-1)
    upper_bound = jnp.broadcast_to(
        jnp.repeat(slot_high, most_rows)[None, :], (kv_count, 2 * most_rows)
    ).reshape(-1)
    sent_rows = incoming.reshape(kv_count * 2 * most_rows, row_width)
    back_rows = 2 * most_rows
    prompt_out, prompt_lse = attend_block(
        sent_rows, prompt_keys, shared_prompt_values, lower_bound, upper_bound, first_position
    )
    returned_out, returned_lse = (
        lax.all_to_all(
            prompt_out.reshape(kv_count, back_rows, row_width),
            "kv",
            split_axis=0,
            concat_axis=0,
            tiled=True,
        ),
        lax.all_to_all(
            prompt_lse.reshape(kv_count, back_rows, heads_local),
            "kv",
            split_axis=0,
            concat_axis=0,
            tiled=True,
        ),
    )
    page_slots = page_table.shape[1]
    page_length = suffix_pool_keys.shape[1]
    suffix_span = page_slots * page_length
    gathered_keys = suffix_pool_keys[page_table].reshape(seq_local, suffix_span, -1)
    gathered_values = suffix_pool_values[page_table].reshape(seq_local, suffix_span, -1)
    suffix_first = sub_index * suffix_span

    def one_sequence(query_line, seq_keys, seq_values, seq_length):
        return attend_block(
            query_line[None, :],
            seq_keys,
            seq_values,
            jnp.zeros((1,), jnp.int32),
            seq_length[None],
            suffix_first,
        )

    suffix_out, suffix_lse = jax.vmap(one_sequence)(
        queries, gathered_keys, gathered_values, suffix_len
    )
    suffix_out = suffix_out[:, 0].reshape(seq_local, heads_local, HEAD_SIZE)
    suffix_lse = suffix_lse[:, 0]
    flat_lse = returned_lse.reshape(-1, heads_local)
    flat_out = returned_out.reshape(-1, heads_local, HEAD_SIZE)
    masked_lse = jnp.where(selector[:, :, None], flat_lse[:, None, :], NEGATIVE)
    joint_max = jnp.maximum(jnp.max(masked_lse, axis=0), suffix_lse)
    factors = jnp.where(selector[:, :, None], jnp.exp(masked_lse - joint_max[None]), 0.0)
    own_factor = jnp.exp(suffix_lse - joint_max)
    totals = jnp.sum(factors, axis=0) + own_factor
    blended = jnp.einsum("rsh,rhd->shd", factors, flat_out, precision=lax.Precision.HIGHEST)
    blended = blended + own_factor[:, :, None] * suffix_out
    joint_max, totals, blended = joined((joint_max, totals, blended), "sub", combine_halves)
    return (blended / totals[:, :, None]).reshape(seq_local, row_width).astype(jnp.float32)


SENT = jnp.int16
STEPS = 32000.0
TINY = 1e-30
LOG2E = 1.4426950408889634
FIRST_SLOT = (0, 0, 1, 1)
HOLDERS = (((0, 0), (1, 0)), ((1, 1), (2, 0), (3, 0)))
CHUNK = 4
SENDS = ((2, 0), (3, 0), (4, 0), (5, 0), (0, 0), (1, 0), (6, 0), (7, 0), (2, 1), (3, 1))


def windows(chip):
    return (0, 1) if chip == 1 else (FIRST_SLOT[chip],)


def lanes(column, width=HEAD_SIZE):
    return jnp.broadcast_to(column, (column.shape[0], width))


def attend(
    prompt_of, prompt_len, suffix_len, page_table,
    q_ref, pk_ref, pv_ref, sk_ref, sv_ref,
    out_ref,
    order, places, qf, q_send, q_all, kbuf, vbuf, pool_k, pool_v,
    o_send, l_send, o_recv, l_recv, l_cols, suf_o, suf_l, merged,
    own_sem, swap_send, swap_recv, pool_sem, qs_sem, qr_sem, os_sem, or_sem, ls_sem, lr_sem,
):
    me = lax.axis_index("kv")
    chip = me // 2
    core = me % 2
    other = 1 - core
    partner = chip * 2 + other
    devices = 8
    rows = q_ref.shape[0]
    most = rows // 2
    heads = pk_ref.shape[1] // HEAD_SIZE
    half = heads // 2
    group = q_ref.shape[1] // (heads * HEAD_SIZE)
    positions = pk_ref.shape[0]
    lines = group * most
    slots = page_table.shape[0]
    span = slots * sk_ref.shape[1]
    scale = LOG2E / math.sqrt(HEAD_SIZE)

    def columns(head):
        return pl.ds(pl.multiple_of(head * HEAD_SIZE, HEAD_SIZE), HEAD_SIZE)

    own_copies = []
    for h in range(half):
        for i, (ref, buf) in enumerate(((pk_ref, kbuf), (pv_ref, vbuf))):
            own_copies.append(pltpu.make_async_copy(
                ref.at[:, columns(core * half + h)], buf.at[core, h], own_sem.at[2 * h + i]))
    for copy in own_copies:
        copy.start()

    pool_copies = [pltpu.make_async_copy(sk_ref, pool_k, pool_sem.at[0]),
                   pltpu.make_async_copy(sv_ref, pool_v, pool_sem.at[1])]
    for copy in pool_copies:
        copy.start()

    barrier = pltpu.get_barrier_semaphore()
    for dst in range(devices):
        @pl.when(me != dst)
        def _():
            pl.semaphore_signal(barrier, inc=1, device_id={"kv": dst},
                                device_id_type=pl.DeviceIdType.MESH)

    count = [jnp.int32(0), jnp.int32(0)]
    place = []
    for s in range(rows):
        is_one = prompt_of[me * rows + s]
        place.append(jnp.where(is_one == 1, most + count[1], count[0]))
        count[0] = count[0] + (1 - is_one)
        count[1] = count[1] + is_one
        places[s] = place[s]
    row_ids = lax.broadcasted_iota(jnp.int32, (rows, rows), 0)
    col_ids = lax.broadcasted_iota(jnp.int32, (rows, rows), 1)
    chooser = jnp.zeros((rows, rows), jnp.float32)
    for s in range(rows):
        chooser = jnp.where((row_ids == place[s]) & (col_ids == s), 1.0, chooser)
    for r in range(rows):
        found = jnp.int32(0)
        for s in range(rows):
            found = jnp.where(place[s] == r, s, found)
        order[r] = found
    chooser = chooser.astype(jnp.bfloat16)
    for h in range(heads):
        width = group * HEAD_SIZE
        block = jnp.dot(chooser, q_ref[:, h * width:(h + 1) * width],
                        preferred_element_type=jnp.float32)
        for p in range(2):
            tall = jnp.concatenate(
                [block[p * most:(p + 1) * most, g * HEAD_SIZE:(g + 1) * HEAD_SIZE]
                 for g in range(group)], axis=0)
            qf[p, h] = tall
            q_send[p, h] = tall.astype(jnp.bfloat16)

    pl.semaphore_wait(barrier, devices - 1)

    def query_copy(dst, slot, src):
        c, d = dst // 2, dst % 2
        prompt = windows(c)[slot]
        return pltpu.make_async_remote_copy(
            src_ref=q_send.at[prompt, pl.ds(d * half, half)], dst_ref=q_all.at[slot, src],
            send_sem=qs_sem.at[dst, slot], recv_sem=qr_sem.at[src, slot],
            device_id={"kv": dst}, device_id_type=pl.DeviceIdType.MESH)

    for dst, slot in SENDS:
        @pl.when(me != dst)
        def _():
            query_copy(dst, slot, me).start()

        @pl.when(me == dst)
        def _():
            q_all[slot, me] = q_send[windows(dst // 2)[slot], (dst % 2) * half:(dst % 2 + 1) * half]

    def swap_copies():
        made = []
        for h in range(half):
            for i, (ref, buf) in enumerate(((pk_ref, kbuf), (pv_ref, vbuf))):
                made.append(pltpu.make_async_remote_copy(
                    src_ref=ref.at[:, columns(other * half + h)], dst_ref=buf.at[core, h],
                    send_sem=swap_send.at[2 * h + i], recv_sem=swap_recv.at[2 * h + i],
                    device_id={"kv": partner}, device_id_type=pl.DeviceIdType.MESH))
        return made

    swaps = swap_copies()
    for copy in swaps:
        copy.start()

    for copy in own_copies:
        copy.wait()
    for copy in swaps:
        copy.wait_recv()

    first_end = prompt_len[0]
    second_end = first_end + prompt_len[1]

    def wait_query(src, slot):
        pltpu.make_async_remote_copy(
            src_ref=q_send.at[0, pl.ds(0, half)], dst_ref=q_all.at[slot, src],
            send_sem=qs_sem.at[src, slot], recv_sem=qr_sem.at[src, slot],
            device_id={"kv": src}, device_id_type=pl.DeviceIdType.MESH).wait_recv()

    side = me // CHUNK

    def back_copies(dst, slot, sender):
        return (
            pltpu.make_async_remote_copy(
                src_ref=o_send.at[slot, dst], dst_ref=o_recv.at[slot, sender],
                send_sem=os_sem.at[dst, slot], recv_sem=or_sem.at[sender, slot],
                device_id={"kv": dst}, device_id_type=pl.DeviceIdType.MESH),
            pltpu.make_async_remote_copy(
                src_ref=l_send.at[slot, dst], dst_ref=l_recv.at[slot, sender],
                send_sem=ls_sem.at[dst, slot], recv_sem=lr_sem.at[sender, slot],
                device_id={"kv": dst}, device_id_type=pl.DeviceIdType.MESH))

    def prompt_slot(slot, low, high, first_block):
        blocks = 2 - first_block
        spot = (chip * 2 + first_block) * positions + lax.broadcasted_iota(
            jnp.int32, (1, blocks * positions), 1)
        bias = jnp.where((spot >= low) & (spot < high), 0.0, NEGATIVE)
        is_level = lax.broadcasted_iota(jnp.int32, (CHUNK * lines, HEAD_SIZE), 1) % 8 < 4

        @pl.loop(0, devices // CHUNK)
        def _(turn):
            near = (turn == 0) if slot == 0 else (turn == 1)
            begin = jnp.where(near, side, 1 - side) * CHUNK

            @pl.loop(0, CHUNK)
            def _(offset):
                src = begin + offset

                @pl.when(me != src)
                def _():
                    wait_query(src, slot)

            @pl.loop(0, half, unroll=2)
            def _(h):
                query = q_all[slot, pl.ds(begin, CHUNK), h].reshape(CHUNK * lines, HEAD_SIZE)
                keys = kbuf[first_block:2, h].reshape(blocks * positions, HEAD_SIZE)
                values = vbuf[first_block:2, h].reshape(blocks * positions, HEAD_SIZE)
                scores = lax.dot_general(query, keys, (((1,), (1,)), ((), ())),
                                         preferred_element_type=jnp.float32)
                scores = scores * scale + bias
                top = jnp.max(scores, axis=1, keepdims=True)
                weights = jnp.exp2(scores - top)
                total = jnp.sum(weights, axis=1, keepdims=True)
                mixed = jnp.dot(weights.astype(jnp.bfloat16), values,
                                preferred_element_type=jnp.float32)
                peak = jnp.maximum(jnp.max(jnp.abs(mixed), axis=1, keepdims=True), TINY)
                steps = jnp.round(mixed * (STEPS / peak)).astype(jnp.int32)
                o_send[slot, pl.ds(begin, CHUNK), h] = steps.astype(SENT).reshape(
                    CHUNK, lines, HEAD_SIZE)
                peak = peak * (1.0 / (STEPS * total))
                facts = jnp.where(is_level, lanes(top + jnp.log2(total)), lanes(peak))
                l_cols[pl.ds(begin, CHUNK), h] = facts.reshape(CHUNK, lines, HEAD_SIZE)

            @pl.loop(0, CHUNK)
            def _(offset):
                dst = begin + offset
                turned = l_cols[dst].reshape(half * lines, HEAD_SIZE).T
                l_send[slot, dst] = turned[0:8]

                @pl.when(me != dst)
                def _():
                    for copy in back_copies(dst, slot, me):
                        copy.start()

                @pl.when(me == dst)
                def _():
                    o_recv[slot, me] = o_send[slot, dst]
                    l_recv[slot, me] = l_send[slot, dst]

    prompt_slot(0, jnp.where(chip < 2, 0, first_end), jnp.where(chip < 2, first_end, second_end), 0)

    @pl.when(chip == 1)
    def _():
        prompt_slot(1, first_end, second_end, 1)

    for copy in pool_copies:
        copy.wait()
    suffix_spot = lax.broadcasted_iota(jnp.int32, (1, span), 1)
    zero = jnp.zeros((group, HEAD_SIZE), jnp.float32)

    @pl.loop(0, rows, unroll=4)
    def _(r):
        s = order[r]
        p, rank = r // most, r % most
        every = pl.ds(rank, group, stride=most)
        wide = []
        for h in range(heads):
            piece = qf[p, h, every, :]
            wide.append(jnp.concatenate([zero] * h + [piece] + [zero] * (heads - 1 - h), axis=1))
        query = jnp.concatenate(wide, axis=0).astype(jnp.bfloat16)
        keys = jnp.concatenate([pool_k[page_table[j, s]] for j in range(slots)], axis=0)
        values = jnp.concatenate([pool_v[page_table[j, s]] for j in range(slots)], axis=0)
        scores = lax.dot_general(query, keys, (((1,), (1,)), ((), ())),
                                 preferred_element_type=jnp.float32)
        scores = scores * scale + jnp.where(suffix_spot < suffix_len[s], 0.0, NEGATIVE)
        top = jnp.max(scores, axis=1, keepdims=True)
        weights = jnp.exp2(scores - top)
        total = jnp.sum(weights, axis=1, keepdims=True)
        mixed = jnp.dot(weights.astype(jnp.bfloat16), values, preferred_element_type=jnp.float32)
        inverse = 1.0 / total
        lse = top + jnp.log2(total)
        for h in range(heads):
            low = h * group
            suf_o[p, h, every, :] = (
                mixed[low:low + group, h * HEAD_SIZE:(h + 1) * HEAD_SIZE] * inverse[low:low + group])
            suf_l[p, h, every, :] = lanes(lse[low:low + group])

    for p in range(2):
        for d in range(2):
            arrived, levels = [], []
            for c, slot in HOLDERS[p]:
                sender = 2 * c + d

                @pl.when(me != sender)
                def _():
                    for copy in back_copies(sender, slot, sender):
                        copy.wait_recv()

                facts = l_recv[slot, sender]
                facts = jnp.concatenate([facts] * (HEAD_SIZE // 8), axis=0).T
                levels.append((lanes(facts[:, 0:1]), lanes(facts[:, 4:5])))
                arrived.append((slot, sender))
            for hh in range(half):
                h = d * half + hh
                mine = slice(hh * lines, (hh + 1) * lines)
                parts = [(level[mine], o_recv[slot, sender, hh].astype(jnp.int32).astype(jnp.float32)
                          * step[mine])
                         for (level, step), (slot, sender) in zip(levels, arrived)]
                parts.append((suf_l[p, h], suf_o[p, h]))
                joint = functools.reduce(jnp.maximum, [level for level, _ in parts])
                factors = [jnp.exp2(level - joint) for level, _ in parts]
                total = functools.reduce(jnp.add, factors)
                blend = functools.reduce(jnp.add, [f * o for f, (_, o) in zip(factors, parts)])
                blend = blend / total
                for g in range(group):
                    first = (h * group + g) * HEAD_SIZE
                    merged[p * most:(p + 1) * most, first:first + HEAD_SIZE] = (
                        blend[g * most:(g + 1) * most])

    for s in range(rows):
        out_ref[s:s + 1, :] = merged[pl.ds(places[s], 1), :]

    for copy in swaps:
        copy.wait_send()


    for dst in range(devices):
        @pl.when(me != dst)
        def _():
            for slot in range(len(windows(dst // 2))):
                query_copy(dst, slot, me).wait_send()

        @pl.when(me != dst)
        def _():
            for copy in back_copies(dst, 0, me):
                copy.wait_send()

        @pl.when((me != dst) & (chip == 1))
        def _():
            for copy in back_copies(dst, 1, me):
                copy.wait_send()


def fused(
    queries,
    prompt_of,
    prompt_len,
    suffix_len,
    page_table,
    prompt_keys,
    shared_prompt_values,
    suffix_pool_keys,
    suffix_pool_values,
):
    rows, width = queries.shape
    most = rows // 2
    positions, depth = prompt_keys.shape
    heads = depth // HEAD_SIZE
    half = heads // 2
    group = width // depth
    lines = group * most
    devices = lax.axis_size("kv")
    f32, bf16 = jnp.float32, jnp.bfloat16
    vmem, dma = pltpu.VMEM, pltpu.SemaphoreType.DMA
    return pl.pallas_call(
        attend,
        out_shape=jax.ShapeDtypeStruct((rows, width), f32),
        in_specs=[pl.BlockSpec(memory_space=pltpu.SMEM)] * 4
        + [pl.BlockSpec(memory_space=pltpu.VMEM)]
        + [pl.BlockSpec(memory_space=pl.ANY)] * 4,
        out_specs=pl.BlockSpec(memory_space=pltpu.VMEM),
        scratch_shapes=[
            pltpu.SMEM((rows,), jnp.int32),
            pltpu.SMEM((rows,), jnp.int32),
            vmem((2, heads, lines, HEAD_SIZE), f32),
            vmem((2, heads, lines, HEAD_SIZE), bf16),
            vmem((2, devices, half, lines, HEAD_SIZE), bf16),
            vmem((2, half, positions, HEAD_SIZE), bf16),
            vmem((2, half, positions, HEAD_SIZE), bf16),
            vmem(suffix_pool_keys.shape, bf16),
            vmem(suffix_pool_values.shape, bf16),
            vmem((2, devices, half, lines, HEAD_SIZE), SENT),
            vmem((2, devices, 8, HEAD_SIZE), f32),
            vmem((2, devices, half, lines, HEAD_SIZE), SENT),
            vmem((2, devices, 8, HEAD_SIZE), f32),
            vmem((devices, half, lines, HEAD_SIZE), f32),
            vmem((2, heads, lines, HEAD_SIZE), f32),
            vmem((2, heads, lines, HEAD_SIZE), f32),
            vmem((rows, width), f32),
            dma((2 * half,)),
            dma((2 * half,)),
            dma((2 * half,)),
            dma((2,)),
            dma((devices, 2)),
            dma((devices, 2)),
            dma((devices, 2)),
            dma((devices, 2)),
            dma((devices, 2)),
            dma((devices, 2)),
        ],
        compiler_params=pltpu.CompilerParams(
            collective_id=0, has_side_effects=True, vmem_limit_bytes=60 * 1024 * 1024
        ),
    )(
        prompt_of.reshape(-1), prompt_len, suffix_len, page_table.T,
        queries, prompt_keys, shared_prompt_values, suffix_pool_keys, suffix_pool_values,
    )


def fits(mesh):
    return mesh.shape["kv"] == 8 and mesh.shape["sub"] == 1


def solution(mesh):
    body = fused if fits(mesh) else shards
    placed = (
        P(("grp", "kv"), "hd"),
        P("grp", None),
        P("grp"),
        P(("grp", "kv")),
        P(("grp", "kv"), "sub"),
        P(("grp", "kv", "sub"), "hd"),
        P(("grp", "kv", "sub"), "hd"),
        P(("grp", "kv", "sub"), None, "hd"),
        P(("grp", "kv", "sub"), None, "hd"),
    )
    return jax.shard_map(
        body, mesh=mesh, in_specs=placed, out_specs=P(("grp", "kv"), "hd"), check_vma=False
    )
```

profile of v0, /device:TPU:0, one launch (start us, length us, event | category | flops | bytes accessed | tf_op | source)
XLA Modules:
  0.0 28.2 jit_solution(11953302619134525237)
XLA Ops:
  0.0 26.5 %shard_map.91 = f32[16,4096]{1,0:T(8,128)} custom-call(s32[128]{0:T(128)} %bitcast.3, s32[2]{0:T(128)} %prompt_len.1, s32[16]{0:T(128)} %suffix_len.1, s32[8,16]{1,0:T(8,128)} %bitcast.2, bf16[16,4096]{1,0:T(8,128)(2,1)} %q_ref.1, bf16[1024,512]{1,0:T(8,128)(2,1)} %pk_ref.1, bf16[1024,512]{1,0:T(8,128)(2,1)} %pv_ref.1, bf16[128,64,512]{2,1,0:T(8,128)(2,1)} %sk_ref.1, ...), custom_call_target="tpu_custom_call" | custom-call | tf_op jit(solution)/shard_map/pallas_call | solution.py:524
  26.5 1.7 %copy.11 = f32[16,4096]{1,0:T(8,128)} copy(f32[16,4096]{1,0:T(8,128)} %shard_map.91) | data formatting | bytes 524288
where the time goes:
time: 28.6 us; the launch traced here: 28.2 us
  Pallas kernels  26.5 us (93%)
  local copies, waits for them, and re-layouts  1.67 us (6%)
    pallas_call x1, Pallas kernels, fused(): pl.pallas_call(attend, out_shape=jax.ShapeDtypeStruct((rows, width), f32)...  26.5 us
    unnamed x1, local copies, waits for them, and re-layouts  1.67 us

commit v1 on v0

--- a/solution.py
+++ b/solution.py
@@ -523,7 +523,7 @@
     vmem, dma = pltpu.VMEM, pltpu.SemaphoreType.DMA
     return pl.pallas_call(
         attend,
-        out_shape=jax.ShapeDtypeStruct((rows, width), f32),
+        out_shape=pltpu.VMEM((rows, width), f32),
         in_specs=[pl.BlockSpec(memory_space=pltpu.SMEM)] * 4
         + [pl.BlockSpec(memory_space=pltpu.VMEM)]
         + [pl.BlockSpec(memory_space=pl.ANY)] * 4,
@@ -558,11 +558,12 @@
             dma((devices, 2)),
         ],
         compiler_params=pltpu.CompilerParams(
-            collective_id=0, has_side_effects=True, vmem_limit_bytes=60 * 1024 * 1024
+            collective_id=0, has_side_effects=True, vmem_limit_bytes=48 * 1024 * 1024
         ),
     )(
-        prompt_of.reshape(-1), prompt_len, suffix_len, page_table.T,
-        queries, prompt_keys, shared_prompt_values, suffix_pool_keys, suffix_pool_values,
+        *(pltpu.with_memory_space_constraint(array, pltpu.HBM) for array in (
+            prompt_of.reshape(-1), prompt_len, suffix_len, page_table.T,
+            queries, prompt_keys, shared_prompt_values, suffix_pool_keys, suffix_pool_values))
     )
 
 

time: 28.6 us -> 26.9 us (0.941)
  local copies, waits for them, and re-layouts: 1.67 us -> 0.71 us
  Pallas kernels: 26.5 us -> 25.8 us
    unnamed x1, local copies, waits for them, and re-layouts: 1.67 us -> 0.71 us
    pallas_call x1, Pallas kernels: 26.5 us -> 25.8 us  [fused(): pl.pallas_call(attend, out_shape=pltpu.VMEM((rows, width), f32), in_specs...]
where the time goes in v1:
time: 26.9 us; the launch traced here: 26.5 us
  Pallas kernels  25.8 us (96%)
  local copies, waits for them, and re-layouts  0.71 us (3%)
    pallas_call x1, Pallas kernels, fused(): pl.pallas_call(attend, out_shape=pltpu.VMEM((rows, width), f32), in_specs...  25.8 us
    unnamed x1, local copies, waits for them, and re-layouts  0.71 us

profile of v1, /device:TPU:0, one launch (start us, length us, event | category | flops | bytes accessed | tf_op | source)
XLA Modules:
  0.0 26.5 jit_solution(358162575296727939)
XLA Ops:
  0.0 25.8 %shard_map.91 = f32[16,4096]{1,0:T(8,128)S(1)} custom-call(s32[128]{0:T(128)} %bitcast.3, s32[2]{0:T(128)} %prompt_len.1, s32[16]{0:T(128)} %suffix_len.1, s32[8,16]{1,0:T(8,128)} %bitcast.2, bf16[16,4096]{1,0:T(8,128)(2,1)} %q_ref.1, bf16[1024,512]{1,0:T(8,128)(2,1)} %pk_ref.1, bf16[1024,512]{1,0:T(8,128)(2,1)} %pv_ref.1, bf16[128,64,512]{2,1,0:T(8,128)(2,1)} %sk_ref.1, ...), custom_call_target="tpu_custom_call" | custom-call | tf_op jit(solution)/shard_map/pallas_call | solution.py:524
  25.8 0.7 %copy.11 = f32[16,4096]{1,0:T(8,128)} copy(f32[16,4096]{1,0:T(8,128)S(1)} %shard_map.91) | data formatting | bytes 524288

commit v2 on v1

--- a/solution.py
+++ b/solution.py
@@ -200,7 +200,7 @@
 FIRST_SLOT = (0, 0, 1, 1)
 HOLDERS = (((0, 0), (1, 0)), ((1, 1), (2, 0), (3, 0)))
 CHUNK = 4
-SENDS = ((2, 0), (3, 0), (4, 0), (5, 0), (0, 0), (1, 0), (6, 0), (7, 0), (2, 1), (3, 1))
+SENDS = ((2, 0), (3, 0), (2, 1), (3, 1), (0, 0), (1, 0), (4, 0), (5, 0), (6, 0), (7, 0))
 
 
 def windows(chip):
@@ -211,13 +211,17 @@
     return jnp.broadcast_to(column, (column.shape[0], width))
 
 
+def standing(row):
+    return jnp.broadcast_to(row, (HEAD_SIZE, HEAD_SIZE)).T
+
+
 def attend(
-    prompt_of, prompt_len, suffix_len, page_table,
-    q_ref, pk_ref, pv_ref, sk_ref, sv_ref,
+    of_ref, len_ref, suf_ref, table_ref, q_in, pk_ref, pv_ref, sk_ref, sv_ref,
     out_ref,
-    order, places, qf, q_send, q_all, kbuf, vbuf, pool_k, pool_v,
-    o_send, l_send, o_recv, l_recv, l_cols, suf_o, suf_l, merged,
-    own_sem, swap_send, swap_recv, pool_sem, qs_sem, qr_sem, os_sem, or_sem, ls_sem, lr_sem,
+    prompt_of, prompt_len, suffix_len, page_table, q_ref, order, places, qf, q_send, q_all, kbuf, vbuf, pool_k, pool_v,
+    o_send, l_send, o_recv, l_recv, l_cols, suf_w, suf_s, suf_o, suf_l, merged,
+    in_sem, own_sem, swap_send, swap_recv, pool_sem, qs_sem, qr_sem, os_sem, or_sem, ls_sem, lr_sem,
+    ready_sem,
 ):
     me = lax.axis_index("kv")
     chip = me // 2
@@ -239,25 +243,53 @@
     def columns(head):
         return pl.ds(pl.multiple_of(head * HEAD_SIZE, HEAD_SIZE), HEAD_SIZE)
 
+    def signal(semaphore, dst):
+        pl.semaphore_signal(semaphore, inc=1, device_id={"kv": dst},
+                            device_id_type=pl.DeviceIdType.MESH)
+
+    barrier = pltpu.get_barrier_semaphore()
+    for dst in range(devices):
+        @pl.when((dst == partner) | (dst // 2 > chip))
+        def _():
+            signal(barrier, dst)
+
+    pool_copies = [pltpu.make_async_copy(sk_ref, pool_k, pool_sem.at[0]),
+                   pltpu.make_async_copy(sv_ref, pool_v, pool_sem.at[1])]
     own_copies = []
     for h in range(half):
         for i, (ref, buf) in enumerate(((pk_ref, kbuf), (pv_ref, vbuf))):
             own_copies.append(pltpu.make_async_copy(
                 ref.at[:, columns(core * half + h)], buf.at[core, h], own_sem.at[2 * h + i]))
+    inputs = [pltpu.make_async_copy(src, dst, in_sem.at[i]) for i, (src, dst) in enumerate((
+        (of_ref, prompt_of), (len_ref, prompt_len), (suf_ref, suffix_len),
+        (table_ref, page_table), (q_in, q_ref)))]
+    for copy in inputs:
+        copy.start()
+    pool_copies[0].start()
     for copy in own_copies:
         copy.start()
-
-    pool_copies = [pltpu.make_async_copy(sk_ref, pool_k, pool_sem.at[0]),
-                   pltpu.make_async_copy(sv_ref, pool_v, pool_sem.at[1])]
-    for copy in pool_copies:
+    pl.semaphore_wait(barrier, 2 * chip + 1)
+    for dst in range(devices):
+        @pl.when(dst // 2 < chip)
+        def _():
+            signal(ready_sem.at[chip], dst)
+
+    def swap_copies():
+        made = []
+        for h in range(half):
+            for i, (ref, buf) in enumerate(((pk_ref, kbuf), (pv_ref, vbuf))):
+                made.append(pltpu.make_async_remote_copy(
+                    src_ref=ref.at[:, columns(other * half + h)], dst_ref=buf.at[core, h],
+                    send_sem=swap_send.at[2 * h + i], recv_sem=swap_recv.at[2 * h + i],
+                    device_id={"kv": partner}, device_id_type=pl.DeviceIdType.MESH))
+        return made
+
+    swaps = swap_copies()
+    for copy in swaps:
         copy.start()
 
-    barrier = pltpu.get_barrier_semaphore()
-    for dst in range(devices):
-        @pl.when(me != dst)
-        def _():
-            pl.semaphore_signal(barrier, inc=1, device_id={"kv": dst},
-                                device_id_type=pl.DeviceIdType.MESH)
+    for copy in inputs:
+        copy.wait()
 
     count = [jnp.int32(0), jnp.int32(0)]
     place = []
@@ -278,6 +310,7 @@
             found = jnp.where(place[s] == r, s, found)
         order[r] = found
     chooser = chooser.astype(jnp.bfloat16)
+
     for h in range(heads):
         width = group * HEAD_SIZE
         block = jnp.dot(chooser, q_ref[:, h * width:(h + 1) * width],
@@ -289,18 +322,21 @@
             qf[p, h] = tall
             q_send[p, h] = tall.astype(jnp.bfloat16)
 
-    pl.semaphore_wait(barrier, devices - 1)
-
     def query_copy(dst, slot, src):
-        c, d = dst // 2, dst % 2
-        prompt = windows(c)[slot]
+        prompt = windows(dst // 2)[slot]
         return pltpu.make_async_remote_copy(
-            src_ref=q_send.at[prompt, pl.ds(d * half, half)], dst_ref=q_all.at[slot, src],
+            src_ref=q_send.at[prompt, pl.ds(dst % 2 * half, half)], dst_ref=q_all.at[slot, src],
             send_sem=qs_sem.at[dst, slot], recv_sem=qr_sem.at[src, slot],
             device_id={"kv": dst}, device_id_type=pl.DeviceIdType.MESH)
 
+    def send_up(to):
+        pl.semaphore_wait(ready_sem.at[to], 2)
+        for dst, slot in SENDS:
+            if dst // 2 == to:
+                query_copy(dst, slot, me).start()
+
     for dst, slot in SENDS:
-        @pl.when(me != dst)
+        @pl.when((me != dst) & (dst // 2 <= chip))
         def _():
             query_copy(dst, slot, me).start()
 
@@ -308,19 +344,62 @@
         def _():
             q_all[slot, me] = q_send[windows(dst // 2)[slot], (dst % 2) * half:(dst % 2 + 1) * half]
 
-    def swap_copies():
-        made = []
-        for h in range(half):
-            for i, (ref, buf) in enumerate(((pk_ref, kbuf), (pv_ref, vbuf))):
-                made.append(pltpu.make_async_remote_copy(
-                    src_ref=ref.at[:, columns(other * half + h)], dst_ref=buf.at[core, h],
-                    send_sem=swap_send.at[2 * h + i], recv_sem=swap_recv.at[2 * h + i],
-                    device_id={"kv": partner}, device_id_type=pl.DeviceIdType.MESH))
-        return made
-
-    swaps = swap_copies()
-    for copy in swaps:
-        copy.start()
+    @pl.when(chip == 0)
+    def _():
+        send_up(1)
+
+    @pl.when(chip == 1)
+    def _():
+        send_up(2)
+
+    @pl.when((chip == 1) | (chip == 2))
+    def _():
+        send_up(3)
+
+    spots = lax.broadcasted_iota(jnp.int32, (span, HEAD_SIZE), 0)
+    lane = lax.broadcasted_iota(jnp.int32, (1, HEAD_SIZE), 1)
+    pairs = heads // 2
+
+    def gathered(pool, s, columns_of):
+        return jnp.concatenate(
+            [pool[page_table[j, s], :, columns_of] for j in range(slots)], axis=0)
+
+    pool_copies[0].wait()
+    pool_copies[1].start()
+
+    def suffix_scores(batch):
+        p, pair = batch // pairs, batch % pairs
+        wanted = pl.ds(pl.multiple_of(pair * 2 * HEAD_SIZE, 2 * HEAD_SIZE), 2 * HEAD_SIZE)
+        tall = qf[p, pl.ds(pair * 2, 2)].reshape(2 * lines, HEAD_SIZE).T.astype(jnp.bfloat16)
+        scores = None
+        length = jnp.zeros((1, HEAD_SIZE), jnp.int32)
+        for rank in range(most):
+            s = order[p * most + rank]
+            mine = lane % most == rank
+            length = jnp.where(mine, suffix_len[s], length)
+            both = [jnp.where(mine & (lane // lines == i), 1.0, 0.0).astype(jnp.bfloat16)
+                    for i in range(2)]
+            query = jnp.concatenate([tall * both[0], tall * both[1]], axis=0)
+            part = jnp.dot(gathered(pool_k, s, wanted), query, preferred_element_type=jnp.float32)
+            scores = part if scores is None else scores + part
+        scores = jnp.where(spots < length, scores * scale, NEGATIVE)
+        top = jnp.max(scores, axis=0, keepdims=True)
+        weights = jnp.exp2(scores - top)
+        total = jnp.sum(weights, axis=0, keepdims=True)
+        suf_w[batch] = weights.T.astype(jnp.bfloat16)
+        suf_s[batch, 0:1] = top + jnp.log2(total)
+        suf_s[batch, 1:2] = 1.0 / total
+
+    @pl.loop(0, 2)
+    def _(p):
+        for pair in range(pairs):
+            suffix_scores(p * pairs + pair)
+
+        @pl.when((chip == 0) & (p == 0))
+        def _():
+            for to in (2, 3):
+                send_up(to)
+
 
     for copy in own_copies:
         copy.wait()
@@ -335,8 +414,6 @@
             src_ref=q_send.at[0, pl.ds(0, half)], dst_ref=q_all.at[slot, src],
             send_sem=qs_sem.at[src, slot], recv_sem=qr_sem.at[src, slot],
             device_id={"kv": src}, device_id_type=pl.DeviceIdType.MESH).wait_recv()
-
-    side = me // CHUNK
 
     def back_copies(dst, slot, sender):
         return (
@@ -349,100 +426,96 @@
                 send_sem=ls_sem.at[dst, slot], recv_sem=lr_sem.at[sender, slot],
                 device_id={"kv": dst}, device_id_type=pl.DeviceIdType.MESH))
 
-    def prompt_slot(slot, low, high, first_block):
+    is_level = lax.broadcasted_iota(jnp.int32, (CHUNK * lines, HEAD_SIZE), 1) % 2 == 0
+
+    def prompt_turn(slot, turn, low, high, first_block):
         blocks = 2 - first_block
         spot = (chip * 2 + first_block) * positions + lax.broadcasted_iota(
             jnp.int32, (1, blocks * positions), 1)
         bias = jnp.where((spot >= low) & (spot < high), 0.0, NEGATIVE)
-        is_level = lax.broadcasted_iota(jnp.int32, (CHUNK * lines, HEAD_SIZE), 1) % 8 < 4
-
-        @pl.loop(0, devices // CHUNK)
-        def _(turn):
-            near = (turn == 0) if slot == 0 else (turn == 1)
-            begin = jnp.where(near, side, 1 - side) * CHUNK
-
-            @pl.loop(0, CHUNK)
-            def _(offset):
-                src = begin + offset
-
-                @pl.when(me != src)
-                def _():
-                    wait_query(src, slot)
-
-            @pl.loop(0, half, unroll=2)
-            def _(h):
-                query = q_all[slot, pl.ds(begin, CHUNK), h].reshape(CHUNK * lines, HEAD_SIZE)
-                keys = kbuf[first_block:2, h].reshape(blocks * positions, HEAD_SIZE)
-                values = vbuf[first_block:2, h].reshape(blocks * positions, HEAD_SIZE)
-                scores = lax.dot_general(query, keys, (((1,), (1,)), ((), ())),
-                                         preferred_element_type=jnp.float32)
-                scores = scores * scale + bias
-                top = jnp.max(scores, axis=1, keepdims=True)
-                weights = jnp.exp2(scores - top)
-                total = jnp.sum(weights, axis=1, keepdims=True)
-                mixed = jnp.dot(weights.astype(jnp.bfloat16), values,
-                                preferred_element_type=jnp.float32)
-                peak = jnp.maximum(jnp.max(jnp.abs(mixed), axis=1, keepdims=True), TINY)
-                steps = jnp.round(mixed * (STEPS / peak)).astype(jnp.int32)
-                o_send[slot, pl.ds(begin, CHUNK), h] = steps.astype(SENT).reshape(
-                    CHUNK, lines, HEAD_SIZE)
-                peak = peak * (1.0 / (STEPS * total))
-                facts = jnp.where(is_level, lanes(top + jnp.log2(total)), lanes(peak))
-                l_cols[pl.ds(begin, CHUNK), h] = facts.reshape(CHUNK, lines, HEAD_SIZE)
-
-            @pl.loop(0, CHUNK)
-            def _(offset):
-                dst = begin + offset
-                turned = l_cols[dst].reshape(half * lines, HEAD_SIZE).T
-                l_send[slot, dst] = turned[0:8]
-
-                @pl.when(me != dst)
-                def _():
-                    for copy in back_copies(dst, slot, me):
-                        copy.start()
-
-                @pl.when(me == dst)
-                def _():
-                    o_recv[slot, me] = o_send[slot, dst]
-                    l_recv[slot, me] = l_send[slot, dst]
-
-    prompt_slot(0, jnp.where(chip < 2, 0, first_end), jnp.where(chip < 2, first_end, second_end), 0)
-
-    @pl.when(chip == 1)
-    def _():
-        prompt_slot(1, first_end, second_end, 1)
-
-    for copy in pool_copies:
-        copy.wait()
-    suffix_spot = lax.broadcasted_iota(jnp.int32, (1, span), 1)
-    zero = jnp.zeros((group, HEAD_SIZE), jnp.float32)
-
-    @pl.loop(0, rows, unroll=4)
-    def _(r):
-        s = order[r]
-        p, rank = r // most, r % most
-        every = pl.ds(rank, group, stride=most)
-        wide = []
-        for h in range(heads):
-            piece = qf[p, h, every, :]
-            wide.append(jnp.concatenate([zero] * h + [piece] + [zero] * (heads - 1 - h), axis=1))
-        query = jnp.concatenate(wide, axis=0).astype(jnp.bfloat16)
-        keys = jnp.concatenate([pool_k[page_table[j, s]] for j in range(slots)], axis=0)
-        values = jnp.concatenate([pool_v[page_table[j, s]] for j in range(slots)], axis=0)
-        scores = lax.dot_general(query, keys, (((1,), (1,)), ((), ())),
-                                 preferred_element_type=jnp.float32)
-        scores = scores * scale + jnp.where(suffix_spot < suffix_len[s], 0.0, NEGATIVE)
-        top = jnp.max(scores, axis=1, keepdims=True)
-        weights = jnp.exp2(scores - top)
-        total = jnp.sum(weights, axis=1, keepdims=True)
-        mixed = jnp.dot(weights.astype(jnp.bfloat16), values, preferred_element_type=jnp.float32)
-        inverse = 1.0 / total
-        lse = top + jnp.log2(total)
-        for h in range(heads):
-            low = h * group
-            suf_o[p, h, every, :] = (
-                mixed[low:low + group, h * HEAD_SIZE:(h + 1) * HEAD_SIZE] * inverse[low:low + group])
-            suf_l[p, h, every, :] = lanes(lse[low:low + group])
+        begin = turn * CHUNK
+
+        @pl.loop(0, CHUNK)
+        def _(offset):
+            src = begin + offset
+
+            @pl.when(me != src)
+            def _():
+                wait_query(src, slot)
+
+        @pl.loop(0, half, unroll=2)
+        def _(h):
+            query = q_all[slot, pl.ds(begin, CHUNK), h].reshape(CHUNK * lines, HEAD_SIZE)
+            keys = kbuf[first_block:2, h].reshape(blocks * positions, HEAD_SIZE)
+            values = vbuf[first_block:2, h].reshape(blocks * positions, HEAD_SIZE)
+            scores = lax.dot_general(query, keys, (((1,), (1,)), ((), ())),
+                                     preferred_element_type=jnp.float32)
+            scores = scores * scale + bias
+            top = jnp.max(scores, axis=1, keepdims=True)
+            weights = jnp.exp2(scores - top)
+            total = jnp.sum(weights, axis=1, keepdims=True)
+            mixed = jnp.dot(weights.astype(jnp.bfloat16), values,
+                            preferred_element_type=jnp.float32)
+            peak = jnp.maximum(jnp.max(jnp.abs(mixed), axis=1, keepdims=True), TINY)
+            steps = jnp.round(mixed * (STEPS / peak)).astype(jnp.int32)
+            o_send[slot, pl.ds(begin, CHUNK), h] = steps.astype(SENT).reshape(
+                CHUNK, lines, HEAD_SIZE)
+            peak = peak * (1.0 / (STEPS * total))
+            facts = jnp.where(is_level, lanes(top + jnp.log2(total)), lanes(peak))
+            l_cols[pl.ds(begin, CHUNK), h] = facts.reshape(CHUNK, lines, HEAD_SIZE)
+
+        @pl.loop(0, CHUNK)
+        def _(offset):
+            dst = begin + offset
+            turned = l_cols[dst].reshape(half * lines, HEAD_SIZE).T
+            l_send[slot, dst] = turned[0:2]
+
+            @pl.when(me != dst)
+            def _():
+                for copy in back_copies(dst, slot, me):
+                    copy.start()
+
+            @pl.when(me == dst)
+            def _():
+                o_recv[slot, me] = o_send[slot, dst]
+                l_recv[slot, me] = l_send[slot, dst]
+
+    low, high = jnp.where(chip < 2, 0, first_end), jnp.where(chip < 2, first_end, second_end)
+    row = lax.broadcasted_iota(jnp.int32, (2 * lines, HEAD_SIZE), 0)
+    late = jnp.where(chip == 1, 1, 0)
+
+    @pl.loop(0, devices // CHUNK)
+    def _(step):
+        turn = jnp.where(chip == 1, 1 - step, step)
+        prompt_turn(0, turn, low, high, 0)
+
+        @pl.when(chip == 1)
+        def _():
+            prompt_turn(1, turn, first_end, second_end, 1)
+
+        @pl.when(step == late)
+        def _():
+            pool_copies[1].wait()
+
+            @pl.loop(0, 2 * pairs)
+            def _(batch):
+                p, pair = batch // pairs, batch % pairs
+                wanted = pl.ds(pl.multiple_of(pair * 2 * HEAD_SIZE, 2 * HEAD_SIZE), 2 * HEAD_SIZE)
+                weights = suf_w[batch]
+                mixed = None
+                for rank in range(most):
+                    s = order[p * most + rank]
+                    mine = jnp.where(row % most == rank, 1.0, 0.0).astype(jnp.bfloat16)
+                    mine = jnp.concatenate([mine] * (span // HEAD_SIZE), axis=1)
+                    part = jnp.dot(weights * mine, gathered(pool_v, s, wanted),
+                                   preferred_element_type=jnp.float32)
+                    mixed = part if mixed is None else mixed + part
+                level, inverse = standing(suf_s[batch, 0:1]), standing(suf_s[batch, 1:2])
+                for i in range(2):
+                    mine = slice(i * lines, (i + 1) * lines)
+                    suf_o[p, pair * 2 + i] = (
+                        mixed[mine, i * HEAD_SIZE:(i + 1) * HEAD_SIZE] * inverse[mine])
+                    suf_l[p, pair * 2 + i] = level[mine]
 
     for p in range(2):
         for d in range(2):
@@ -455,9 +528,7 @@
                     for copy in back_copies(sender, slot, sender):
                         copy.wait_recv()
 
-                facts = l_recv[slot, sender]
-                facts = jnp.concatenate([facts] * (HEAD_SIZE // 8), axis=0).T
-                levels.append((lanes(facts[:, 0:1]), lanes(facts[:, 4:5])))
+                levels.append((standing(l_recv[slot, sender, 0:1]), standing(l_recv[slot, sender, 1:2])))
                 arrived.append((slot, sender))
             for hh in range(half):
                 h = d * half + hh
@@ -482,13 +553,12 @@
     for copy in swaps:
         copy.wait_send()
 
+    for dst, slot in SENDS:
+        @pl.when((me != dst))
+        def _():
+            query_copy(dst, slot, me).wait_send()
 
     for dst in range(devices):
-        @pl.when(me != dst)
-        def _():
-            for slot in range(len(windows(dst // 2))):
-                query_copy(dst, slot, me).wait_send()
-
         @pl.when(me != dst)
         def _():
             for copy in back_copies(dst, 0, me):
@@ -518,17 +588,21 @@
     half = heads // 2
     group = width // depth
     lines = group * most
+    span = page_table.shape[1] * suffix_pool_keys.shape[1]
     devices = lax.axis_size("kv")
     f32, bf16 = jnp.float32, jnp.bfloat16
     vmem, dma = pltpu.VMEM, pltpu.SemaphoreType.DMA
     return pl.pallas_call(
         attend,
         out_shape=pltpu.VMEM((rows, width), f32),
-        in_specs=[pl.BlockSpec(memory_space=pltpu.SMEM)] * 4
-        + [pl.BlockSpec(memory_space=pltpu.VMEM)]
-        + [pl.BlockSpec(memory_space=pl.ANY)] * 4,
+        in_specs=[pl.BlockSpec(memory_space=pl.ANY)] * 9,
         out_specs=pl.BlockSpec(memory_space=pltpu.VMEM),
         scratch_shapes=[
+            pltpu.SMEM(prompt_of.shape[:1], jnp.int32),
+            pltpu.SMEM(prompt_len.shape, jnp.int32),
+            pltpu.SMEM(suffix_len.shape, jnp.int32),
+            pltpu.SMEM(page_table.shape[::-1], jnp.int32),
+            vmem((rows, width), bf16),
             pltpu.SMEM((rows,), jnp.int32),
             pltpu.SMEM((rows,), jnp.int32),
             vmem((2, heads, lines, HEAD_SIZE), f32),
@@ -539,13 +613,16 @@
             vmem(suffix_pool_keys.shape, bf16),
             vmem(suffix_pool_values.shape, bf16),
             vmem((2, devices, half, lines, HEAD_SIZE), SENT),
-            vmem((2, devices, 8, HEAD_SIZE), f32),
+            vmem((2, devices, 2, HEAD_SIZE), f32),
             vmem((2, devices, half, lines, HEAD_SIZE), SENT),
-            vmem((2, devices, 8, HEAD_SIZE), f32),
+            vmem((2, devices, 2, HEAD_SIZE), f32),
             vmem((devices, half, lines, HEAD_SIZE), f32),
+            vmem((heads, 2 * lines, span), bf16),
+            vmem((heads, 2, HEAD_SIZE), f32),
             vmem((2, heads, lines, HEAD_SIZE), f32),
             vmem((2, heads, lines, HEAD_SIZE), f32),
             vmem((rows, width), f32),
+            dma((5,)),
             dma((2 * half,)),
             dma((2 * half,)),
             dma((2 * half,)),
@@ -556,6 +633,7 @@
             dma((devices, 2)),
             dma((devices, 2)),
             dma((devices, 2)),
+            pltpu.SemaphoreType.REGULAR((devices // 2,)),
         ],
         compiler_params=pltpu.CompilerParams(
             collective_id=0, has_side_effects=True, vmem_limit_bytes=48 * 1024 * 1024

time: 26.9 us -> 24.8 us (0.922)
  Pallas kernels: 25.8 us -> 23.9 us
    pallas_call x1, Pallas kernels: 25.8 us -> 23.9 us  [fused(): pl.pallas_call(attend, out_shape=pltpu.VMEM((rows, width), f32), in_specs...]
where the time goes in v2:
time: 24.8 us; the launch traced here: 24.6 us
  Pallas kernels  23.9 us (96%)
  local copies, waits for them, and re-layouts  0.71 us (3%)
    pallas_call x1, Pallas kernels, fused(): pl.pallas_call(attend, out_shape=pltpu.VMEM((rows, width), f32), in_specs...  23.9 us
    unnamed x1, local copies, waits for them, and re-layouts  0.71 us

profile of v2, /device:TPU:0, one launch (start us, length us, event | category | flops | bytes accessed | tf_op | source)
XLA Modules:
  0.0 24.6 jit_solution(8709025501096621319)
XLA Ops:
  0.0 23.9 %shard_map.91 = f32[16,4096]{1,0:T(8,128)S(1)} custom-call(s32[128]{0:T(128)} %bitcast.3, s32[2]{0:T(128)} %len_ref.1, s32[16]{0:T(128)} %suf_ref.1, s32[8,16]{1,0:T(8,128)} %bitcast.2, bf16[16,4096]{1,0:T(8,128)(2,1)} %q_in.1, bf16[1024,512]{1,0:T(8,128)(2,1)} %pk_ref.1, bf16[1024,512]{1,0:T(8,128)(2,1)} %pv_ref.1, bf16[128,64,512]{2,1,0:T(8,128)(2,1)} %sk_ref.1, ...), custom_call_target="tpu_custom_call" | custom-call | tf_op jit(solution)/shard_map/pallas_call | solution.py:595
  23.9 0.7 %copy.11 = f32[16,4096]{1,0:T(8,128)} copy(f32[16,4096]{1,0:T(8,128)S(1)} %shard_map.91) | data formatting | bytes 524288

commit v3 on v2

--- a/solution.py
+++ b/solution.py
@@ -200,7 +200,7 @@
 FIRST_SLOT = (0, 0, 1, 1)
 HOLDERS = (((0, 0), (1, 0)), ((1, 1), (2, 0), (3, 0)))
 CHUNK = 4
-SENDS = ((2, 0), (3, 0), (2, 1), (3, 1), (0, 0), (1, 0), (4, 0), (5, 0), (6, 0), (7, 0))
+SENDS = ((2, 0), (3, 0), (0, 0), (1, 0), (2, 1), (3, 1), (4, 0), (5, 0), (6, 0), (7, 0))
 
 
 def windows(chip):
@@ -221,7 +221,7 @@
     prompt_of, prompt_len, suffix_len, page_table, q_ref, order, places, qf, q_send, q_all, kbuf, vbuf, pool_k, pool_v,
     o_send, l_send, o_recv, l_recv, l_cols, suf_w, suf_s, suf_o, suf_l, merged,
     in_sem, own_sem, swap_send, swap_recv, pool_sem, qs_sem, qr_sem, os_sem, or_sem, ls_sem, lr_sem,
-    ready_sem,
+    relay_sem, ready_sem, held, held_top,
 ):
     me = lax.axis_index("kv")
     chip = me // 2
@@ -336,7 +336,7 @@
                 query_copy(dst, slot, me).start()
 
     for dst, slot in SENDS:
-        @pl.when((me != dst) & (dst // 2 <= chip))
+        @pl.when((me != dst) & (dst // 2 <= chip) & ((chip < 2) | ((slot == 0) & (dst > 1))))
         def _():
             query_copy(dst, slot, me).start()
 
@@ -366,6 +366,12 @@
 
     pool_copies[0].wait()
     pool_copies[1].start()
+
+    @pl.when(chip >= 2)
+    def _():
+        for dst, slot in SENDS:
+            if slot == 1:
+                query_copy(dst, slot, me).start()
 
     def suffix_scores(batch):
         p, pair = batch // pairs, batch % pairs
@@ -390,16 +396,18 @@
         suf_s[batch, 0:1] = top + jnp.log2(total)
         suf_s[batch, 1:2] = 1.0 / total
 
-    @pl.loop(0, 2)
-    def _(p):
+    def suffix_half(p):
         for pair in range(pairs):
             suffix_scores(p * pairs + pair)
 
+    @pl.loop(0, jnp.where(chip == 1, 1, 2))
+    def _(p):
+        suffix_half(p)
+
         @pl.when((chip == 0) & (p == 0))
         def _():
             for to in (2, 3):
                 send_up(to)
-
 
     for copy in own_copies:
         copy.wait()
@@ -415,16 +423,27 @@
             send_sem=qs_sem.at[src, slot], recv_sem=qr_sem.at[src, slot],
             device_id={"kv": src}, device_id_type=pl.DeviceIdType.MESH).wait_recv()
 
+    def relay_copy(offset):
+        src = CHUNK + offset
+        return pltpu.make_async_remote_copy(
+            src_ref=q_all.at[0, src], dst_ref=q_all.at[0, src],
+            send_sem=relay_sem.at[offset], recv_sem=qr_sem.at[src, 0],
+            device_id={"kv": core}, device_id_type=pl.DeviceIdType.MESH)
+
+    def head_copy(dst, slot, sender, h):
+        return pltpu.make_async_remote_copy(
+            src_ref=o_send.at[slot, dst, h], dst_ref=o_recv.at[slot, sender, h],
+            send_sem=os_sem.at[dst, slot, h], recv_sem=or_sem.at[sender, slot, h],
+            device_id={"kv": dst}, device_id_type=pl.DeviceIdType.MESH)
+
+    def facts_copy(dst, slot, sender):
+        return pltpu.make_async_remote_copy(
+            src_ref=l_send.at[slot, dst], dst_ref=l_recv.at[slot, sender],
+            send_sem=ls_sem.at[dst, slot], recv_sem=lr_sem.at[sender, slot],
+            device_id={"kv": dst}, device_id_type=pl.DeviceIdType.MESH)
+
     def back_copies(dst, slot, sender):
-        return (
-            pltpu.make_async_remote_copy(
-                src_ref=o_send.at[slot, dst], dst_ref=o_recv.at[slot, sender],
-                send_sem=os_sem.at[dst, slot], recv_sem=or_sem.at[sender, slot],
-                device_id={"kv": dst}, device_id_type=pl.DeviceIdType.MESH),
-            pltpu.make_async_remote_copy(
-                src_ref=l_send.at[slot, dst], dst_ref=l_recv.at[slot, sender],
-                send_sem=ls_sem.at[dst, slot], recv_sem=lr_sem.at[sender, slot],
-                device_id={"kv": dst}, device_id_type=pl.DeviceIdType.MESH))
+        return [head_copy(dst, slot, sender, h) for h in range(half)] + [facts_copy(dst, slot, sender)]
 
     is_level = lax.broadcasted_iota(jnp.int32, (CHUNK * lines, HEAD_SIZE), 1) % 2 == 0
 
@@ -439,20 +458,23 @@
         def _(offset):
             src = begin + offset
 
-            @pl.when(me != src)
+            @pl.when((me != src) & ((chip != 1) | (turn == 0) | (slot == 1)))
             def _():
                 wait_query(src, slot)
 
-        @pl.loop(0, half, unroll=2)
-        def _(h):
+        width = blocks * positions
+
+        def scored(h):
             query = q_all[slot, pl.ds(begin, CHUNK), h].reshape(CHUNK * lines, HEAD_SIZE)
-            keys = kbuf[first_block:2, h].reshape(blocks * positions, HEAD_SIZE)
-            values = vbuf[first_block:2, h].reshape(blocks * positions, HEAD_SIZE)
+            keys = kbuf[first_block:2, h].reshape(width, HEAD_SIZE)
             scores = lax.dot_general(query, keys, (((1,), (1,)), ((), ())),
                                      preferred_element_type=jnp.float32)
             scores = scores * scale + bias
-            top = jnp.max(scores, axis=1, keepdims=True)
-            weights = jnp.exp2(scores - top)
+            return scores, lanes(jnp.max(scores, axis=1, keepdims=True))
+
+        def finished(h, scores, top):
+            values = vbuf[first_block:2, h].reshape(width, HEAD_SIZE)
+            weights = jnp.exp2(scores - jnp.concatenate([top] * (width // HEAD_SIZE), axis=1))
             total = jnp.sum(weights, axis=1, keepdims=True)
             mixed = jnp.dot(weights.astype(jnp.bfloat16), values,
                             preferred_element_type=jnp.float32)
@@ -461,8 +483,32 @@
             o_send[slot, pl.ds(begin, CHUNK), h] = steps.astype(SENT).reshape(
                 CHUNK, lines, HEAD_SIZE)
             peak = peak * (1.0 / (STEPS * total))
-            facts = jnp.where(is_level, lanes(top + jnp.log2(total)), lanes(peak))
+            facts = jnp.where(is_level, top + lanes(jnp.log2(total)), lanes(peak))
             l_cols[pl.ds(begin, CHUNK), h] = facts.reshape(CHUNK, lines, HEAD_SIZE)
+
+        def returned(h):
+            @pl.loop(0, CHUNK)
+            def _(offset):
+                @pl.when(me != begin + offset)
+                def _():
+                    head_copy(begin + offset, slot, me, h).start()
+
+        ready = scored(0)
+        for h in range(half):
+            finished(h, *ready)
+            if h + 1 < half:
+                scores, top = scored(h + 1)
+                held[:, :width] = scores
+                held_top[...] = top
+            if slot == 1 and h == 0:
+                @pl.when(turn == 0)
+                def _():
+                    for i in range(CHUNK):
+                        wait_query(CHUNK + i, 0)
+                        relay_copy(i).start()
+            returned(h)
+            if h + 1 < half:
+                ready = (held[:, :width], held_top[...])
 
         @pl.loop(0, CHUNK)
         def _(offset):
@@ -472,8 +518,7 @@
 
             @pl.when(me != dst)
             def _():
-                for copy in back_copies(dst, slot, me):
-                    copy.start()
+                facts_copy(dst, slot, me).start()
 
             @pl.when(me == dst)
             def _():
@@ -482,40 +527,45 @@
 
     low, high = jnp.where(chip < 2, 0, first_end), jnp.where(chip < 2, first_end, second_end)
     row = lax.broadcasted_iota(jnp.int32, (2 * lines, HEAD_SIZE), 0)
-    late = jnp.where(chip == 1, 1, 0)
-
-    @pl.loop(0, devices // CHUNK)
+
+    def suffix_values():
+        pool_copies[1].wait()
+
+        @pl.loop(0, 2 * pairs)
+        def _(batch):
+            p, pair = batch // pairs, batch % pairs
+            wanted = pl.ds(pl.multiple_of(pair * 2 * HEAD_SIZE, 2 * HEAD_SIZE), 2 * HEAD_SIZE)
+            weights = suf_w[batch]
+            mixed = None
+            for rank in range(most):
+                s = order[p * most + rank]
+                mine = jnp.where(row % most == rank, 1.0, 0.0).astype(jnp.bfloat16)
+                mine = jnp.concatenate([mine] * (span // HEAD_SIZE), axis=1)
+                part = jnp.dot(weights * mine, gathered(pool_v, s, wanted),
+                               preferred_element_type=jnp.float32)
+                mixed = part if mixed is None else mixed + part
+            level, inverse = standing(suf_s[batch, 0:1]), standing(suf_s[batch, 1:2])
+            for i in range(2):
+                mine = slice(i * lines, (i + 1) * lines)
+                suf_o[p, pair * 2 + i] = (
+                    mixed[mine, i * HEAD_SIZE:(i + 1) * HEAD_SIZE] * inverse[mine])
+                suf_l[p, pair * 2 + i] = level[mine]
+
+    @pl.loop(0, 2)
     def _(step):
-        turn = jnp.where(chip == 1, 1 - step, step)
-        prompt_turn(0, turn, low, high, 0)
-
         @pl.when(chip == 1)
         def _():
-            prompt_turn(1, turn, first_end, second_end, 1)
-
-        @pl.when(step == late)
-        def _():
-            pool_copies[1].wait()
-
-            @pl.loop(0, 2 * pairs)
-            def _(batch):
-                p, pair = batch // pairs, batch % pairs
-                wanted = pl.ds(pl.multiple_of(pair * 2 * HEAD_SIZE, 2 * HEAD_SIZE), 2 * HEAD_SIZE)
-                weights = suf_w[batch]
-                mixed = None
-                for rank in range(most):
-                    s = order[p * most + rank]
-                    mine = jnp.where(row % most == rank, 1.0, 0.0).astype(jnp.bfloat16)
-                    mine = jnp.concatenate([mine] * (span // HEAD_SIZE), axis=1)
-                    part = jnp.dot(weights * mine, gathered(pool_v, s, wanted),
-                                   preferred_element_type=jnp.float32)
-                    mixed = part if mixed is None else mixed + part
-                level, inverse = standing(suf_s[batch, 0:1]), standing(suf_s[batch, 1:2])
-                for i in range(2):
-                    mine = slice(i * lines, (i + 1) * lines)
-                    suf_o[p, pair * 2 + i] = (
-                        mixed[mine, i * HEAD_SIZE:(i + 1) * HEAD_SIZE] * inverse[mine])
-                    suf_l[p, pair * 2 + i] = level[mine]
+            prompt_turn(1, step, first_end, second_end, 1)
+
+        prompt_turn(0, jnp.where(chip == 1, 1 - step, step), low, high, 0)
+
+        @pl.when((chip == 1) & (step == 1))
+        def _():
+            suffix_half(1)
+
+        @pl.when(step == jnp.where(chip == 1, 1, 0))
+        def _():
+            suffix_values()
 
     for p in range(2):
         for d in range(2):
@@ -554,9 +604,14 @@
         copy.wait_send()
 
     for dst, slot in SENDS:
-        @pl.when((me != dst))
+        @pl.when((me != dst) & ((chip < 2) | (dst > 1)))
         def _():
             query_copy(dst, slot, me).wait_send()
+
+    @pl.when(chip == 1)
+    def _():
+        for i in range(CHUNK):
+            relay_copy(i).wait_send()
 
     for dst in range(devices):
         @pl.when(me != dst)
@@ -629,11 +684,14 @@
             dma((2,)),
             dma((devices, 2)),
             dma((devices, 2)),
+            dma((devices, 2, half)),
+            dma((devices, 2, half)),
             dma((devices, 2)),
             dma((devices, 2)),
-            dma((devices, 2)),
-            dma((devices, 2)),
+            dma((CHUNK,)),
             pltpu.SemaphoreType.REGULAR((devices // 2,)),
+            vmem((CHUNK * lines, 2 * positions), f32),
+            vmem((CHUNK * lines, HEAD_SIZE), f32),
         ],
         compiler_params=pltpu.CompilerParams(
             collective_id=0, has_side_effects=True, vmem_limit_bytes=48 * 1024 * 1024

time: 24.8 us -> 23 us (0.927)
  Pallas kernels: 23.9 us -> 22.1 us
    pallas_call x1, Pallas kernels: 23.9 us -> 22.1 us  [fused(): pl.pallas_call(attend, out_shape=pltpu.VMEM((rows, width), f32), in_specs...]
where the time goes in v3:
time: 23 us; the launch traced here: 22.9 us
  Pallas kernels  22.1 us (96%)
  local copies, waits for them, and re-layouts  0.71 us (3%)
    pallas_call x1, Pallas kernels, fused(): pl.pallas_call(attend, out_shape=pltpu.VMEM((rows, width), f32), in_specs...  22.1 us
    unnamed x1, local copies, waits for them, and re-layouts  0.71 us

profile of v3, /device:TPU:0, one launch (start us, length us, event | category | flops | bytes accessed | tf_op | source)
XLA Modules:
  0.0 22.9 jit_solution(10489581705024495027)
XLA Ops:
  0.0 22.1 %shard_map.91 = f32[16,4096]{1,0:T(8,128)S(1)} custom-call(s32[128]{0:T(128)} %bitcast.3, s32[2]{0:T(128)} %len_ref.1, s32[16]{0:T(128)} %suf_ref.1, s32[8,16]{1,0:T(8,128)} %bitcast.2, bf16[16,4096]{1,0:T(8,128)(2,1)} %q_in.1, bf16[1024,512]{1,0:T(8,128)(2,1)} %pk_ref.1, bf16[1024,512]{1,0:T(8,128)(2,1)} %pv_ref.1, bf16[128,64,512]{2,1,0:T(8,128)(2,1)} %sk_ref.1, ...), custom_call_target="tpu_custom_call" | custom-call | tf_op jit(solution)/shard_map/pallas_call | solution.py:650
  22.2 0.7 %copy.11 = f32[16,4096]{1,0:T(8,128)} copy(f32[16,4096]{1,0:T(8,128)S(1)} %shard_map.91) | data formatting | bytes 524288

commit v4 on v3

--- a/solution.py
+++ b/solution.py
@@ -259,7 +259,7 @@
     for h in range(half):
         for i, (ref, buf) in enumerate(((pk_ref, kbuf), (pv_ref, vbuf))):
             own_copies.append(pltpu.make_async_copy(
-                ref.at[:, columns(core * half + h)], buf.at[core, h], own_sem.at[2 * h + i]))
+                ref.at[:, columns(core * half + h)], buf.at[core, h], own_sem.at[i]))
     inputs = [pltpu.make_async_copy(src, dst, in_sem.at[i]) for i, (src, dst) in enumerate((
         (of_ref, prompt_of), (len_ref, prompt_len), (suf_ref, suffix_len),
         (table_ref, page_table), (q_in, q_ref)))]
@@ -280,7 +280,7 @@
             for i, (ref, buf) in enumerate(((pk_ref, kbuf), (pv_ref, vbuf))):
                 made.append(pltpu.make_async_remote_copy(
                     src_ref=ref.at[:, columns(other * half + h)], dst_ref=buf.at[core, h],
-                    send_sem=swap_send.at[2 * h + i], recv_sem=swap_recv.at[2 * h + i],
+                    send_sem=swap_send.at[i], recv_sem=swap_recv.at[i],
                     device_id={"kv": partner}, device_id_type=pl.DeviceIdType.MESH))
         return made
 
@@ -326,7 +326,7 @@
         prompt = windows(dst // 2)[slot]
         return pltpu.make_async_remote_copy(
             src_ref=q_send.at[prompt, pl.ds(dst % 2 * half, half)], dst_ref=q_all.at[slot, src],
-            send_sem=qs_sem.at[dst, slot], recv_sem=qr_sem.at[src, slot],
+            send_sem=qs_sem.at[slot], recv_sem=qr_sem.at[slot, src // CHUNK],
             device_id={"kv": dst}, device_id_type=pl.DeviceIdType.MESH)
 
     def send_up(to):
@@ -409,41 +409,57 @@
             for to in (2, 3):
                 send_up(to)
 
-    for copy in own_copies:
-        copy.wait()
-    for copy in swaps:
-        copy.wait_recv()
+    def both_heads(i):
+        buf = (kbuf, vbuf)[i]
+        return pltpu.make_async_remote_copy(
+            src_ref=buf.at[core], dst_ref=buf.at[core], send_sem=swap_send.at[i],
+            recv_sem=swap_recv.at[i], device_id={"kv": partner},
+            device_id_type=pl.DeviceIdType.MESH)
+
+    for i, buf in enumerate((kbuf, vbuf)):
+        pltpu.make_async_copy(buf.at[core], buf.at[core], own_sem.at[i]).wait()
+        both_heads(i).wait_recv()
 
     first_end = prompt_len[0]
     second_end = first_end + prompt_len[1]
 
-    def wait_query(src, slot):
-        pltpu.make_async_remote_copy(
-            src_ref=q_send.at[0, pl.ds(0, half)], dst_ref=q_all.at[slot, src],
-            send_sem=qs_sem.at[src, slot], recv_sem=qr_sem.at[src, slot],
-            device_id={"kv": src}, device_id_type=pl.DeviceIdType.MESH).wait_recv()
+    def query_span(slot, turn, number):
+        return pltpu.make_async_remote_copy(
+            src_ref=q_all.at[slot, pl.ds(0, number)], dst_ref=q_all.at[slot, pl.ds(0, number)],
+            send_sem=qs_sem.at[slot], recv_sem=qr_sem.at[slot, turn],
+            device_id={"kv": partner}, device_id_type=pl.DeviceIdType.MESH)
 
     def relay_copy(offset):
         src = CHUNK + offset
         return pltpu.make_async_remote_copy(
             src_ref=q_all.at[0, src], dst_ref=q_all.at[0, src],
-            send_sem=relay_sem.at[offset], recv_sem=qr_sem.at[src, 0],
+            send_sem=relay_sem.at[0], recv_sem=qr_sem.at[0, 1],
             device_id={"kv": core}, device_id_type=pl.DeviceIdType.MESH)
 
-    def head_copy(dst, slot, sender, h):
+    def head_copy(dst, slot, h):
+        group = 2 if slot == 1 else me // CHUNK
         return pltpu.make_async_remote_copy(
-            src_ref=o_send.at[slot, dst, h], dst_ref=o_recv.at[slot, sender, h],
-            send_sem=os_sem.at[dst, slot, h], recv_sem=or_sem.at[sender, slot, h],
+            src_ref=o_send.at[slot, dst, h], dst_ref=o_recv.at[slot, me, h],
+            send_sem=os_sem.at[slot], recv_sem=or_sem.at[group, core],
             device_id={"kv": dst}, device_id_type=pl.DeviceIdType.MESH)
 
-    def facts_copy(dst, slot, sender):
+    def facts_copy(dst, slot):
+        group = 2 if slot == 1 else me // CHUNK
         return pltpu.make_async_remote_copy(
-            src_ref=l_send.at[slot, dst], dst_ref=l_recv.at[slot, sender],
-            send_sem=ls_sem.at[dst, slot], recv_sem=lr_sem.at[sender, slot],
+            src_ref=l_send.at[slot, dst], dst_ref=l_recv.at[slot, me],
+            send_sem=ls_sem.at[slot], recv_sem=lr_sem.at[group, core],
             device_id={"kv": dst}, device_id_type=pl.DeviceIdType.MESH)
 
-    def back_copies(dst, slot, sender):
-        return [head_copy(dst, slot, sender, h) for h in range(half)] + [facts_copy(dst, slot, sender)]
+    def back_spans(slot, group, d, number):
+        return [pltpu.make_async_remote_copy(
+            src_ref=sent.at[slot, pl.ds(0, number)], dst_ref=got.at[slot, pl.ds(0, number)],
+            send_sem=left.at[slot], recv_sem=landed.at[group, d],
+            device_id={"kv": partner}, device_id_type=pl.DeviceIdType.MESH)
+            for sent, got, left, landed in ((o_send, o_recv, os_sem, or_sem), (l_send, l_recv, ls_sem, lr_sem))]
+
+    def wait_back(slot, group, d, number):
+        for span_copy in back_spans(slot, group, d, number):
+            span_copy.wait_recv()
 
     is_level = lax.broadcasted_iota(jnp.int32, (CHUNK * lines, HEAD_SIZE), 1) % 2 == 0
 
@@ -454,13 +470,15 @@
         bias = jnp.where((spot >= low) & (spot < high), 0.0, NEGATIVE)
         begin = turn * CHUNK
 
-        @pl.loop(0, CHUNK)
-        def _(offset):
-            src = begin + offset
-
-            @pl.when((me != src) & ((chip != 1) | (turn == 0) | (slot == 1)))
-            def _():
-                wait_query(src, slot)
+        waits = (chip != 1) | (turn == 0) | (slot == 1)
+
+        @pl.when(me // CHUNK == turn)
+        def _():
+            query_span(slot, turn, CHUNK - 1).wait_recv()
+
+        @pl.when((me // CHUNK != turn) & waits)
+        def _():
+            query_span(slot, turn, CHUNK).wait_recv()
 
         width = blocks * positions
 
@@ -491,7 +509,7 @@
             def _(offset):
                 @pl.when(me != begin + offset)
                 def _():
-                    head_copy(begin + offset, slot, me, h).start()
+                    head_copy(begin + offset, slot, h).start()
 
         ready = scored(0)
         for h in range(half):
@@ -503,8 +521,8 @@
             if slot == 1 and h == 0:
                 @pl.when(turn == 0)
                 def _():
+                    query_span(0, 1, CHUNK).wait_recv()
                     for i in range(CHUNK):
-                        wait_query(CHUNK + i, 0)
                         relay_copy(i).start()
             returned(h)
             if h + 1 < half:
@@ -518,7 +536,7 @@
 
             @pl.when(me != dst)
             def _():
-                facts_copy(dst, slot, me).start()
+                facts_copy(dst, slot).start()
 
             @pl.when(me == dst)
             def _():
@@ -570,14 +588,23 @@
     for p in range(2):
         for d in range(2):
             arrived, levels = [], []
+            if p == 1:
+                @pl.when(me != 2 + d)
+                def _():
+                    wait_back(1, 2, d, 1)
+
+            inside = (me // CHUNK == p) & (core == d)
+
+            @pl.when(inside)
+            def _():
+                wait_back(0, p, d, 1)
+
+            @pl.when(jnp.logical_not(inside))
+            def _():
+                wait_back(0, p, d, 2)
+
             for c, slot in HOLDERS[p]:
                 sender = 2 * c + d
-
-                @pl.when(me != sender)
-                def _():
-                    for copy in back_copies(sender, slot, sender):
-                        copy.wait_recv()
-
                 levels.append((standing(l_recv[slot, sender, 0:1]), standing(l_recv[slot, sender, 1:2])))
                 arrived.append((slot, sender))
             for hh in range(half):
@@ -600,29 +627,33 @@
     for s in range(rows):
         out_ref[s:s + 1, :] = merged[pl.ds(places[s], 1), :]
 
-    for copy in swaps:
-        copy.wait_send()
-
-    for dst, slot in SENDS:
-        @pl.when((me != dst) & ((chip < 2) | (dst > 1)))
-        def _():
-            query_copy(dst, slot, me).wait_send()
+    for i in range(2):
+        both_heads(i).wait_send()
+
+    @pl.when(chip < 2)
+    def _():
+        query_span(0, 0, devices - 1).wait_send()
+
+    @pl.when(chip >= 2)
+    def _():
+        query_span(0, 0, devices - 3).wait_send()
 
     @pl.when(chip == 1)
     def _():
-        for i in range(CHUNK):
-            relay_copy(i).wait_send()
-
-    for dst in range(devices):
-        @pl.when(me != dst)
-        def _():
-            for copy in back_copies(dst, 0, me):
-                copy.wait_send()
-
-        @pl.when((me != dst) & (chip == 1))
-        def _():
-            for copy in back_copies(dst, 1, me):
-                copy.wait_send()
+        query_span(1, 0, 1).wait_send()
+        pltpu.make_async_remote_copy(
+            src_ref=q_all.at[0, pl.ds(CHUNK, CHUNK)], dst_ref=q_all.at[0, pl.ds(CHUNK, CHUNK)],
+            send_sem=relay_sem.at[0], recv_sem=qr_sem.at[0, 1],
+            device_id={"kv": core}, device_id_type=pl.DeviceIdType.MESH).wait_send()
+        for span_copy in back_spans(1, 2, 0, devices - 1):
+            span_copy.wait_send()
+
+    @pl.when(chip != 1)
+    def _():
+        query_span(1, 0, 2).wait_send()
+
+    for span_copy in back_spans(0, 0, 0, devices - 1):
+        span_copy.wait_send()
 
 
 def fused(
@@ -678,17 +709,17 @@
             vmem((2, heads, lines, HEAD_SIZE), f32),
             vmem((rows, width), f32),
             dma((5,)),
-            dma((2 * half,)),
-            dma((2 * half,)),
-            dma((2 * half,)),
             dma((2,)),
-            dma((devices, 2)),
-            dma((devices, 2)),
-            dma((devices, 2, half)),
-            dma((devices, 2, half)),
-            dma((devices, 2)),
-            dma((devices, 2)),
-            dma((CHUNK,)),
+            dma((2,)),
+            dma((2,)),
+            dma((2,)),
+            dma((2,)),
+            dma((2, 2)),
+            dma((2,)),
+            dma((3, 2)),
+            dma((2,)),
+            dma((3, 2)),
+            dma((1,)),
             pltpu.SemaphoreType.REGULAR((devices // 2,)),
             vmem((CHUNK * lines, 2 * positions), f32),
             vmem((CHUNK * lines, HEAD_SIZE), f32),

time: 23 us -> 21.5 us (0.935)
  Pallas kernels: 22.1 us -> 20.6 us
    pallas_call x1, Pallas kernels: 22.1 us -> 20.6 us  [fused(): pl.pallas_call(attend, out_shape=pltpu.VMEM((rows, width), f32), in_specs...]
where the time goes in v4:
time: 21.5 us; the launch traced here: 21.3 us
  Pallas kernels  20.6 us (96%)
  local copies, waits for them, and re-layouts  0.71 us (3%)
    pallas_call x1, Pallas kernels, fused(): pl.pallas_call(attend, out_shape=pltpu.VMEM((rows, width), f32), in_specs...  20.6 us
    unnamed x1, local copies, waits for them, and re-layouts  0.71 us

profile of v4, /device:TPU:0, one launch (start us, length us, event | category | flops | bytes accessed | tf_op | source)
XLA Modules:
  0.0 21.3 jit_solution(10259430069551546381)
XLA Ops:
  0.0 20.6 %shard_map.91 = f32[16,4096]{1,0:T(8,128)S(1)} custom-call(s32[128]{0:T(128)} %bitcast.3, s32[2]{0:T(128)} %len_ref.1, s32[16]{0:T(128)} %suf_ref.1, s32[8,16]{1,0:T(8,128)} %bitcast.2, bf16[16,4096]{1,0:T(8,128)(2,1)} %q_in.1, bf16[1024,512]{1,0:T(8,128)(2,1)} %pk_ref.1, bf16[1024,512]{1,0:T(8,128)(2,1)} %pv_ref.1, bf16[128,64,512]{2,1,0:T(8,128)(2,1)} %sk_ref.1, ...), custom_call_target="tpu_custom_call" | custom-call | tf_op jit(solution)/shard_map/pallas_call | solution.py:681
  20.6 0.7 %copy.11 = f32[16,4096]{1,0:T(8,128)} copy(f32[16,4096]{1,0:T(8,128)S(1)} %shard_map.91) | data formatting | bytes 524288

commit v5 on v4

--- a/solution.py
+++ b/solution.py
@@ -331,7 +331,7 @@
 
     def send_up(to):
         pl.semaphore_wait(ready_sem.at[to], 2)
-        for dst, slot in SENDS:
+        for dst, slot in SENDS[::-1]:
             if dst // 2 == to:
                 query_copy(dst, slot, me).start()
 
@@ -585,7 +585,7 @@
         def _():
             suffix_values()
 
-    for p in range(2):
+    def merge(p):
         for d in range(2):
             arrived, levels = [], []
             if p == 1:
@@ -623,6 +623,16 @@
                     first = (h * group + g) * HEAD_SIZE
                     merged[p * most:(p + 1) * most, first:first + HEAD_SIZE] = (
                         blend[g * most:(g + 1) * most])
+
+    @pl.when(me < CHUNK)
+    def _():
+        merge(1)
+
+    merge(0)
+
+    @pl.when(me >= CHUNK)
+    def _():
+        merge(1)
 
     for s in range(rows):
         out_ref[s:s + 1, :] = merged[pl.ds(places[s], 1), :]

time: 21.5 us -> 21 us (0.977)
  Pallas kernels: 20.6 us -> 20.1 us
    pallas_call x1, Pallas kernels: 20.6 us -> 20.1 us  [fused(): pl.pallas_call(attend, out_shape=pltpu.VMEM((rows, width), f32), in_specs...]
where the time goes in v5:
time: 21 us; the launch traced here: 20.8 us
  Pallas kernels  20.1 us (96%)
  local copies, waits for them, and re-layouts  0.71 us (3%)
    pallas_call x1, Pallas kernels, fused(): pl.pallas_call(attend, out_shape=pltpu.VMEM((rows, width), f32), in_specs...  20.1 us
    unnamed x1, local copies, waits for them, and re-layouts  0.71 us

profile of v5, /device:TPU:0, one launch (start us, length us, event | category | flops | bytes accessed | tf_op | source)
XLA Modules:
  0.0 20.8 jit_solution(5057991314260374038)
XLA Ops:
  0.0 20.1 %shard_map.91 = f32[16,4096]{1,0:T(8,128)S(1)} custom-call(s32[128]{0:T(128)} %bitcast.3, s32[2]{0:T(128)} %len_ref.1, s32[16]{0:T(128)} %suf_ref.1, s32[8,16]{1,0:T(8,128)} %bitcast.2, bf16[16,4096]{1,0:T(8,128)(2,1)} %q_in.1, bf16[1024,512]{1,0:T(8,128)(2,1)} %pk_ref.1, bf16[1024,512]{1,0:T(8,128)(2,1)} %pv_ref.1, bf16[128,64,512]{2,1,0:T(8,128)(2,1)} %sk_ref.1, ...), custom_call_target="tpu_custom_call" | custom-call | tf_op jit(solution)/shard_map/pallas_call | solution.py:691
  20.1 0.7 %copy.11 = f32[16,4096]{1,0:T(8,128)} copy(f32[16,4096]{1,0:T(8,128)S(1)} %shard_map.91) | data formatting | bytes 524288
